TPU v7x, 32 devices: a whole 2x2x4 slice. The times are simulated.
32 devices in a mesh: ao: 8 (over y, x, core), aux: 4 (over z).
Axes of the slice: x: 2, y: 2, z: 4, core: 2. Of those that a mesh axis runs over, the one named last changes fastest.
Arguments:
- blocks: bfloat16 [48, 256, 128, 128], P('ao', 'aux'), may hold values from -6 to 6
- pairs: int32 [48, 2], P('ao'), may hold values from 0 to 79, as said below
- counts: int32 [8], P('ao'), may hold values from 1 to 6, as said below
- owned_blocks: int32 [80], P('ao'), may hold values from 0 to 79, as said below
- occ_coef: bfloat16 [80, 8, 128], P('ao'), may hold values from -0.5 to 0.5
- vir_coef: bfloat16 [10240, 9216], P('ao', 'aux'), may hold values from -0.109375 to 0.109375
Outputs:
- b_tensor: bfloat16 [256, 8, 9216], P('ao', None, 'aux')
Inputs may be any that keep to these rules, and one draw needn't show every extreme that they name: `pairs`: among the used slots of one ao index, at most 3 have nu blocks whose rows one owner holds; in every draw some index reaches 3. `counts`: some ao index uses all 6 slots in every draw. `owned_blocks`: every atom block appears exactly once.
All inputs are finite; a program needn't handle non-finite values.
Results may differ from a plain program's by a relative error of at most 0.014.
Values may be sent and summed in bfloat16 or wider, within the bound.
A program may use at most 128 MiB of HBM per device.

v0:
```python
import jax
import jax.numpy as jnp
from jax import lax
from jax.sharding import PartitionSpec as P


def block_place(block_ids, owned_all):
    hits = block_ids[..., None] == owned_all
    positions = jnp.arange(owned_all.shape[0], dtype=jnp.int32)
    return jnp.sum(jnp.where(hits, positions, 0), axis=-1)


def per_device(blocks, pairs, counts, owned_blocks, occ_coef, vir_coef):
    groups = lax.axis_size("ao")
    own_index = lax.axis_index("ao")
    slot_count = blocks.shape[0]
    aux_depth = blocks.shape[1]
    block_width = blocks.shape[3]
    occupied = occ_coef.shape[1]
    all_pairs, all_counts, all_owned = (
        lax.all_gather(pairs, "ao", axis=0, tiled=True),
        lax.all_gather(counts, "ao", axis=0, tiled=True),
        lax.all_gather(owned_blocks, "ao", axis=0, tiled=True),
    )
    occ_all = lax.all_gather(occ_coef, "ao", axis=0, tiled=True)
    total_blocks = all_owned.shape[0]
    per_owner = total_blocks // groups
    slot_ids = jnp.arange(slot_count, dtype=jnp.int32)
    in_use = slot_ids < counts[0]
    occ_pick = occ_all[block_place(pairs[:, 0], all_owned)]
    slab_values = jnp.einsum("sim,spmn->spin", occ_pick, blocks, preferred_element_type=jnp.float32)
    slab_values = jnp.where(in_use[:, None, None, None], slab_values, 0.0).astype(jnp.bfloat16)
    flat_slabs = slab_values.reshape(slot_count, aux_depth * occupied, block_width)
    place_all = block_place(all_pairs[:, 1], all_owned).reshape(groups, slot_count)
    owner_all = place_all // per_owner
    local_all = place_all % per_owner
    live_all = slot_ids[None, :] < all_counts[:, None]
    mine_all = live_all & (owner_all == own_index)
    local_ids = jnp.arange(per_owner, dtype=jnp.int32)
    slabs_got = lax.all_gather(flat_slabs, "ao", axis=0, tiled=True)
    assign = (
        mine_all.reshape(-1)[None, :] & (local_all.reshape(-1)[None, :] == local_ids[:, None])
    ).astype(jnp.bfloat16)
    summed = jnp.einsum("lt,tqm->qlm", assign, slabs_got, preferred_element_type=jnp.float32)
    rows_local = summed.reshape(summed.shape[0], per_owner * block_width).astype(jnp.bfloat16)
    rows_whole = lax.all_gather(rows_local, "aux", axis=0, tiled=True)
    share = rows_whole.shape[0] // groups
    result = lax.psum_scatter(
        jnp.dot(rows_whole, vir_coef, preferred_element_type=jnp.float32).astype(jnp.bfloat16),
        "ao",
        scatter_dimension=0,
        tiled=True,
    ).astype(jnp.float32)
    return result.reshape(share // occupied, occupied, vir_coef.shape[1]).astype(jnp.bfloat16)


def solution(mesh):
    in_specs = (
        P("ao", "aux", None, None),
        P("ao", None),
        P("ao"),
        P("ao"),
        P("ao", None, None),
        P("ao", "aux"),
    )
    out_specs = P("ao", None, "aux")
    return jax.shard_map(
        per_device, mesh=mesh, in_specs=in_specs, out_specs=out_specs, check_vma=False
    )
```

profile of v0, /device:TPU:0, one launch (start us, length us, event | category | flops | bytes accessed | tf_op | source)
XLA Modules:
  0.0 291.0 jit_solution(9892513670469097050)
XLA Ops:
  7.2 0.7 slice_bitcast_fusion.1
  7.9 1.3 dynamic-slice
  9.9 0.8 dynamic-update-slice.1
  10.7 0.8 dynamic-update-slice
  11.5 9.5 %all-reduce.2 = (s32[80]{0:T(128)S(1)}, s32[8]{0:T(128)S(1)}) all-reduce(s32[80]{0:T(128)S(1)} %dynamic-update-slice, s32[8]{0:T(128)S(1)} %dynamic-update-slice.1), channel_id=1, replica_groups=mesh['ao'=8,'aux'=4] {'ao'}, use_global_device_ids=true, to_apply=%add | all-reduce | flops 88 | bytes 704
  21.0 0.2 select_reduce_fusion.1
  21.2 8.6 %all_gather.18 = bf16[80,8,128]{2,1,0:T(8,128)(2,1)S(1)} all-gather(bf16[10,8,128]{2,1,0:T(8,128)(2,1)} %param.10), channel_id=1, replica_groups=mesh['ao'=8,'aux'=4] {'ao'}, dimensions={0}, use_global_device_ids=true | all-gather | bytes 184320 | tf_op jit(solution)/shard_map/all_gather | solution.py:25
  29.8 0.6 gather_fusion
  30.4 7.2 %fusion.4 = bf16[6,512,128]{2,1,0:T(8,128)(2,1)} fusion(bf16[6,64,128,128]{3,2,1,0:T(8,128)(2,1)} %param.6, pred[6]{0:T(512)(128)(4,1)S(1)} %iota_compare_fusion.2, bf16[6,8,128]{2,1,0:T(8,128)(2,1)S(1)} %gather_fusion), kind=kOutput, calls=%fused_computation.6 | convolution fusion | flops 101449728 | bytes 13381638 | tf_op jit(solution)/shard_map/sim,spmn->spin/dot_general | solution.py:31
  37.6 0.0 all-gather.4.cloned.1.call-update
  37.6 0.0 all-gather.6.cloned.1.call-start
  37.7 0.1 iota_compare_fusion.1
  37.8 0.1 lt.52
  37.9 8.6 %all-gather = s32[8,6,2]{1,2,0:T(2,128)S(1)} all-gather(s32[1,6,2]{1,2,0:T(2,128)S(1)} %bitcast.35), channel_id=1, replica_groups=mesh['ao'=8,'aux'=4] {'ao'}, dimensions={0}, use_global_device_ids=true | all-gather | bytes 432 | tf_op jit(solution)/shard_map/all_gather | solution.py:21
  46.5 0.1 reshape.75
  46.5 0.2 select_reduce_fusion
  46.8 36.7 %all-gather.4.cloned.1.call-done = bf16[48,512,128]{2,1,0:T(8,128)(2,1)} async-done(((bf16[6,512,128]{2,1,0:T(8,128)(2,1)}), bf16[48,512,128]{2,1,0:T(8,128)(2,1)}) %all-gather.4.cloned.1.call-update) | async-done | bytes 6291472 | tf_op jit(solution)/shard_map/all_gather | solution.py:40
  83.5 6.4 %convert_bitcast_fusion = bf16[512,10,128]{2,1,0:T(8,128)(2,1)S(1)} fusion(bf16[48,512,128]{2,1,0:T(8,128)(2,1)} %all-gather.4.cloned.1.call-done, s32[48]{0:T(128)S(1)} %and_select_fusion, pred[48]{0:T(512)(128)(4,1)S(1)} %compare_and_fusion), kind=kOutput, calls=%fused_computation.4 | convolution fusion | flops 63570880 | bytes 7602416 | tf_op jit(solution)/shard_map/lt,tqm->qlm/dot_general | solution.py:44
  89.9 2.6 copy.17
  92.5 0.0 all-gather.6.cloned.1.call-update
  92.5 0.2 reduce-scatter.2.cloned.1.call-start
  92.7 98.0 %all-gather.6.cloned.1.call-done = bf16[2048,1280]{0,1:T(8,128)(2,1)} async-done(((bf16[512,1280]{0,1:T(8,128)(2,1)}), bf16[2048,1280]{0,1:T(8,128)(2,1)}) %all-gather.6.cloned.1.call-update) | async-done | bytes 5242896 | tf_op jit(solution)/shard_map/all_gather | solution.py:46
  190.7 18.4 %convolution_convert_fusion = bf16[2048,2304]{1,0:T(8,128)(2,1)} fusion(bf16[2048,1280]{0,1:T(8,128)(2,1)} %all-gather.6.cloned.1.call-done, bf16[1280,2304]{1,0:T(8,128)(2,1)} %param.11), kind=kOutput, calls=%fused_computation.1 | convolution fusion | flops 12084314112 | bytes 20578304 | tf_op jit(solution)/shard_map/dot_general | solution.py:49
  209.1 75.3 %reduce-scatter.2.cloned.1.call-done = bf16[256,2304]{1,0:T(8,128)(2,1)} async-done(((bf16[2048,2304]{1,0:T(8,128)(2,1)}), bf16[256,2304]{1,0:T(8,128)(2,1)}) %reduce-scatter.2.cloned.1.call-update) | async-done | bytes 1179664 | tf_op jit(solution)/shard_map/reduce_scatter | solution.py:48
  (13 shorter events, 0.1 us)
Async XLA Ops:
  6.5 76.9 %all-gather.4.cloned.1.call-start = ((), (), s32[]{:S(2)}) async-start(), calls=%async_computation.1 | async-start | bytes 7077888 | tf_op jit(solution)/shard_map/all_gather | solution.py:40
  30.4 7.5 %copy-start = (s32[6,2]{0,1:T(2,128)S(1)}, s32[6,2]{0,1:T(2,128)}, u32[]{:S(2)}) copy-start(s32[6,2]{0,1:T(2,128)} %param.7) | copy-start | bytes 148
  37.6 153.0 %all-gather.6.cloned.1.call-start = ((), (), s32[]{:S(2)}) async-start(), calls=%async_computation.2 | async-start | bytes 6553600 | tf_op jit(solution)/shard_map/all_gather | solution.py:46
  92.5 191.9 %reduce-scatter.2.cloned.1.call-start = ((), (), s32[]{:S(2)}) async-start(), calls=%async_computation.3 | async-start | bytes 10616832 | tf_op jit(solution)/shard_map/reduce_scatter | solution.py:48
Sparse Core Ops, SparseCore 0:
  37.8 45.6 all-gather.3
  92.6 98.0 all-gather.5
  209.2 75.1 reduce-scatter.1
where the time goes:
time: 291 us
  waiting for transfers between devices  210 us (72%)
  matrix products  32.1 us (11%)
  blocking collectives  26.7 us (9%)
  between operations  14.5 us (5%)
  local copies, waits for them, and re-layouts  6.95 us (2%)
    all_gather x1, waiting for transfers between devices, per_device(): rows_whole = lax.all_gather(rows_local, 'aux', axis=0, tiled=True)  98 us
    reduce_scatter x1, waiting for transfers between devices, per_device(): lax.psum_scatter(jnp.dot(rows_whole, vir_coef, preferred_element_type=jnp...  75.3 us
    all_gather x1, waiting for transfers between devices, per_device(): slabs_got = lax.all_gather(flat_slabs, 'ao', axis=0, tiled=True)  36.7 us
    dot_general x1, matrix products, per_device(): jnp.dot(rows_whole, vir_coef, preferred_element_type=jnp.float32)  18.4 us
    unnamed x1, blocking collectives  9.49 us
    all_gather x1, blocking collectives, per_device(): occ_all = lax.all_gather(occ_coef, 'ao', axis=0, tiled=True)  8.6 us
    all_gather x1, blocking collectives, per_device(): lax.all_gather(pairs, 'ao', axis=0, tiled=True)  8.59 us
    dot_general x1, matrix products, per_device(): jnp.einsum('sim,spmn->spin', occ_pick, blocks, preferred_element_type=jnp...  7.2 us
  transfers between devices with their start and end apart: 3, of which 3 were waited for; matrix products, arithmetic and copies ran while one was open for 0% of the time, Pallas kernels for 0%

commit v1 on v0

--- a/solution.py
+++ b/solution.py
@@ -1,7 +1,19 @@
+import functools
+
 import jax
 import jax.numpy as jnp
 from jax import lax
+from jax.experimental import pallas as pl
+from jax.experimental.pallas import tpu as pltpu
 from jax.sharding import PartitionSpec as P
+
+MESH = pl.DeviceIdType.MESH
+CAP = 3
+CHUNKS = 4
+
+
+def few_blocks(per_owner):
+    return -(-per_owner * 2 // 3)
 
 
 def block_place(block_ids, owned_all):
@@ -10,7 +22,349 @@
     return jnp.sum(jnp.where(hits, positions, 0), axis=-1)
 
 
+def small_kernel(n, meta_ref, occ_ref, meta_out, occ_out, s_sem, r_sem, l_sem):
+    me = lax.axis_index("ao")
+    barrier = pltpu.get_barrier_semaphore()
+    for k in range(1, n):
+        pl.semaphore_signal(barrier, inc=1, device_id={"ao": lax.rem(me + k, n)}, device_id_type=MESH)
+    own = [
+        pltpu.make_async_copy(meta_ref, meta_out.at[me], l_sem.at[0]),
+        pltpu.make_async_copy(occ_ref, occ_out.at[me], l_sem.at[1]),
+    ]
+    for copy in own:
+        copy.start()
+    pl.semaphore_wait(barrier, n - 1)
+    sent = []
+    for k in range(1, n):
+        for which, (src, dst) in enumerate(((meta_ref, meta_out), (occ_ref, occ_out))):
+            copy = pltpu.make_async_remote_copy(
+                src_ref=src, dst_ref=dst.at[me], send_sem=s_sem.at[which, k], recv_sem=r_sem.at[which, k],
+                device_id={"ao": lax.rem(me + k, n)}, device_id_type=MESH,
+            )
+            copy.start()
+            sent.append(copy)
+    for copy in own + sent:
+        copy.wait()
+
+
+def gather_small(n, meta, occ):
+    return pl.pallas_call(
+        functools.partial(small_kernel, n),
+        out_shape=(
+            jax.ShapeDtypeStruct((n,) + meta.shape, meta.dtype),
+            jax.ShapeDtypeStruct((n,) + occ.shape, occ.dtype),
+        ),
+        in_specs=[pl.BlockSpec(memory_space=pltpu.VMEM)] * 2,
+        out_specs=(pl.BlockSpec(memory_space=pltpu.VMEM),) * 2,
+        scratch_shapes=[
+            pltpu.SemaphoreType.DMA((2, n)),
+            pltpu.SemaphoreType.DMA((2, n)),
+            pltpu.SemaphoreType.DMA((2,)),
+        ],
+        compiler_params=pltpu.CompilerParams(collective_id=0, has_side_effects=True),
+    )(meta, occ)
+
+
+def main_kernel(
+    n, nz, kept, idx_ref, w_ref, pick_ref, half_ref, vir_hbm, out_ref,
+    vir_all, vir, snd, rcv, rows, part, pair, rx, ry, tx, ty,
+    vir_sem, own_sem, a_s, a_r, up_s, up_r, dn_s, dn_r, p_s, p_r, x_s, x_r, y_s, y_r,
+):
+    me, z = lax.axis_index("ao"), lax.axis_index("aux")
+    core, chip = lax.rem(me, 2), me // 2
+    cx, cy = lax.rem(chip, 2), chip // 2
+    mate = me + 1 - 2 * core
+    xmate = me + 2 - 4 * cx
+    ymate = me + 4 - 8 * cy
+    total = n * CAP
+    width = rcv.shape[-1]
+    step = rcv.shape[3]
+    mid = step // 2
+
+    barrier = pltpu.get_barrier_semaphore()
+    for k in range(1, n):
+        pl.semaphore_signal(barrier, inc=1, device_id={"ao": lax.rem(me + k, n)}, device_id_type=MESH)
+    for k in range(1, nz):
+        pl.semaphore_signal(barrier, inc=1, device_id={"aux": lax.rem(z + k, nz)}, device_id_type=MESH)
+    vir_copy = pltpu.make_async_copy(vir_hbm, vir_all, vir_sem)
+    vir_copy.start()
+
+    def pack(i, carry):
+        snd[i] = half_ref[idx_ref[i]]
+        return carry
+
+    lax.fori_loop(0, total, pack, 0)
+    pl.semaphore_wait(barrier, n + nz - 2)
+
+    a_copies = []
+    for c in range(CHUNKS):
+        span = pl.ds(c * step, step)
+        mine = pl.ds(me * CAP, CAP)
+        local = pltpu.make_async_copy(snd.at[mine, :, span, :], rcv.at[c, mine], own_sem.at[c])
+        local.start()
+        group = [local]
+        for k in range(1, n):
+            dst = lax.rem(me + k, n)
+            copy = pltpu.make_async_remote_copy(
+                src_ref=snd.at[pl.ds(dst * CAP, CAP), :, span, :], dst_ref=rcv.at[c, mine],
+                send_sem=a_s.at[c, k], recv_sem=a_r.at[c, k],
+                device_id={"ao": dst}, device_id_type=MESH,
+            )
+            copy.start()
+            group.append(copy)
+        a_copies.append(group)
+
+    def z_copy(c, d, up):
+        src = z - d if up else z + d
+        return pltpu.make_async_remote_copy(
+            src_ref=rows.at[c, src], dst_ref=rows.at[c, src],
+            send_sem=(up_s if up else dn_s).at[c, d], recv_sem=(up_r if up else dn_r).at[c, d],
+            device_id={"aux": z + 1 if up else z - 1}, device_id_type=MESH,
+        )
+
+    def z_send(c, d):
+        @pl.when((z - d >= 0) & (z + 1 < nz))
+        def _():
+            z_copy(c, d, True).start()
+
+        @pl.when((z + d < nz) & (z >= 1))
+        def _():
+            z_copy(c, d, False).start()
+
+    def z_recv(c, d, up):
+        src = z - d if up else z + d
+        return pltpu.make_async_remote_copy(
+            src_ref=rows.at[c, src], dst_ref=rows.at[c, src],
+            send_sem=(up_s if up else dn_s).at[c, d - 1], recv_sem=(up_r if up else dn_r).at[c, d - 1],
+            device_id={"aux": z - 1 if up else z + 1}, device_id_type=MESH,
+        )
+
+    def stage_a(c):
+        a_copies[c][0].wait()
+        for copy in a_copies[c][1:]:
+            copy.wait_recv()
+        for l in range(kept):
+            def add(s, acc):
+                for j in range(CAP):
+                    t = s * CAP + j
+                    acc = acc + w_ref[l * total + t] * rcv[c, t].astype(jnp.float32)
+                return acc
+
+            acc = lax.fori_loop(0, n, add, jnp.zeros((2, step, width), jnp.float32))
+            rows[c, z, :, l * width:(l + 1) * width] = acc.reshape(2 * step, width).astype(jnp.bfloat16)
+        z_send(c, 0)
+
+    def stage_b(c, d):
+        @pl.when(z - d >= 0)
+        def _():
+            z_recv(c, d, True).wait_recv()
+
+        @pl.when(z + d < nz)
+        def _():
+            z_recv(c, d, False).wait_recv()
+
+        if d < nz - 1:
+            z_send(c, d)
+
+    pair_copies, x_copies, y_copies = {}, {}, {}
+
+    def remote(src, dst, ss, rs, to):
+        copy = pltpu.make_async_remote_copy(
+            src_ref=src, dst_ref=dst, send_sem=ss, recv_sem=rs, device_id={"ao": to}, device_id_type=MESH,
+        )
+        copy.start()
+        return copy
+
+    tile = 256
+    depth = rows.shape[-1]
+
+    def stage_m(c):
+        @pl.loop(0, vir.shape[1] // tile)
+        def _(j):
+            cols = pl.ds(pl.multiple_of(j * tile, tile), tile)
+            left = rows[c].reshape(nz * 2 * step, depth)
+            got = jnp.dot(left, vir[:, cols], preferred_element_type=jnp.float32)
+            got = got.astype(jnp.bfloat16).reshape(nz, 2, step, tile)
+            for h in range(2):
+                part[c, h, :, :, cols] = got[:, h]
+
+        pair_copies[c] = remote(part.at[c, 1 - core], pair.at[c], p_s.at[c], p_r.at[c], mate)
+
+    def add2(a, b):
+        return (a.astype(jnp.float32) + b.astype(jnp.float32)).astype(jnp.bfloat16)
+
+    def stage_p(c):
+        pair_copies[c].wait_recv()
+
+        @pl.loop(0, nz)
+        def _(i):
+            pair[c, i] = add2(pair[c, i], part[c, core, i])
+
+        lo, hi = pl.ds(0, mid), pl.ds(mid, mid)
+        x_copies[c] = [
+            remote(pair.at[c, 1 - cx, lo], rx.at[c, 0], x_s.at[c, 0], x_r.at[c, 0], xmate),
+            remote(pair.at[c, 2 * (1 - cy), hi], ry.at[c, 0], y_s.at[c, 0], y_r.at[c, 0], ymate),
+            remote(pair.at[c, 3 - cx, lo], rx.at[c, 1], x_s.at[c, 1], x_r.at[c, 1], xmate),
+            remote(pair.at[c, 2 * (1 - cy) + 1, hi], ry.at[c, 1], y_s.at[c, 1], y_r.at[c, 1], ymate),
+        ]
+
+    def stage_x(c):
+        for copy in x_copies[c]:
+            copy.wait_recv()
+        tx[c] = add2(pair[c, 2 * (1 - cy) + cx, :mid], rx[c, 1 - cy])
+        ty[c] = add2(pair[c, 2 * cy + 1 - cx, mid:], ry[c, 1 - cx])
+        y_copies[c] = [
+            remote(tx.at[c], rx.at[c, 2], y_s.at[c, 2], y_r.at[c, 2], ymate),
+            remote(ty.at[c], ry.at[c, 2], x_s.at[c, 2], x_r.at[c, 2], xmate),
+        ]
+
+    def stage_y(c):
+        for copy in y_copies[c]:
+            copy.wait_recv()
+        f32 = jnp.float32
+        own = pair[c, 2 * cy + cx]
+        top = own[:mid].astype(f32) + rx[c, cy].astype(f32) + rx[c, 2].astype(f32)
+        low = own[mid:].astype(f32) + ry[c, cx].astype(f32) + ry[c, 2].astype(f32)
+        out_ref[c * step:c * step + mid, :] = top.astype(jnp.bfloat16)
+        out_ref[c * step + mid:(c + 1) * step, :] = low.astype(jnp.bfloat16)
+
+    vir_copy.wait()
+    piece = 16
+
+    @pl.loop(0, width // piece)
+    def _(i):
+        at = pl.ds(pl.multiple_of(i * piece, piece), piece)
+        for k in range(kept):
+            to = pl.ds(pl.multiple_of(k * width + i * piece, piece), piece)
+            vir[to, :] = vir_all[pick_ref[k], at, :]
+
+    plan = (
+        "A0 B01 A1 B02", "A2 B11 B03 M0", "A3 B12 B21 P0", "B13 M1 B22 B31",
+        "X0 P1 B23 M2", "B32 Y0 X1 P2", "B33 M3 Y1 X2", "P3 Y2 X3 Y3",
+    )
+    run = {"A": stage_a, "B": stage_b, "M": stage_m, "P": stage_p, "X": stage_x, "Y": stage_y}
+    for item in [name for row in plan for name in row.split()]:
+        run[item[0]](*[int(v) for v in item[1:]])
+
+    for c in range(CHUNKS):
+        for copy in a_copies[c][1:] + [pair_copies[c]] + x_copies[c] + y_copies[c]:
+            copy.wait_send()
+        for d in range(nz - 1):
+            @pl.when((z - d >= 0) & (z + 1 < nz))
+            def _():
+                z_copy(c, d, True).wait_send()
+
+            @pl.when((z + d < nz) & (z >= 1))
+            def _():
+                z_copy(c, d, False).wait_send()
+
+
+def fused(n, nz, kept, call_id, idx, weights, pick, half, vir_coef):
+    _, _, span, width = half.shape
+    step = span // CHUNKS
+    columns = vir_coef.shape[2]
+    bf = jnp.bfloat16
+    dma = pltpu.SemaphoreType.DMA
+    vm = pltpu.VMEM
+    return pl.pallas_call(
+        functools.partial(main_kernel, n, nz, kept),
+        out_shape=jax.ShapeDtypeStruct((span, columns), bf),
+        in_specs=[
+            pl.BlockSpec(memory_space=pltpu.SMEM),
+            pl.BlockSpec(memory_space=pltpu.SMEM),
+            pl.BlockSpec(memory_space=pltpu.SMEM),
+            pl.BlockSpec(memory_space=pltpu.VMEM),
+            pl.BlockSpec(memory_space=pl.ANY),
+        ],
+        out_specs=pl.BlockSpec(memory_space=pltpu.VMEM),
+        scratch_shapes=[
+            vm(vir_coef.shape, bf),
+            vm((kept * width, columns), bf),
+            vm((n * CAP, 2, span, width), bf),
+            vm((CHUNKS, n * CAP, 2, step, width), bf),
+            vm((CHUNKS, nz, 2 * step, kept * width), bf),
+            vm((CHUNKS, 2, nz, step, columns), bf),
+            vm((CHUNKS, nz, step, columns), bf),
+            vm((CHUNKS, 3, step // 2, columns), bf),
+            vm((CHUNKS, 3, step // 2, columns), bf),
+            vm((CHUNKS, step // 2, columns), bf),
+            vm((CHUNKS, step // 2, columns), bf),
+            dma, dma((CHUNKS,)),
+            dma((CHUNKS, n)), dma((CHUNKS, n)),
+            dma((CHUNKS, nz)), dma((CHUNKS, nz)), dma((CHUNKS, nz)), dma((CHUNKS, nz)),
+            dma((CHUNKS,)), dma((CHUNKS,)),
+            dma((CHUNKS, 3)), dma((CHUNKS, 3)), dma((CHUNKS, 3)), dma((CHUNKS, 3)),
+        ],
+        compiler_params=pltpu.CompilerParams(
+            collective_id=call_id, has_side_effects=True, vmem_limit_bytes=62 * 1024 * 1024,
+        ),
+    )(idx, weights, pick, half, vir_coef)
+
+
 def per_device(blocks, pairs, counts, owned_blocks, occ_coef, vir_coef):
+    groups, nz = lax.axis_size("ao"), lax.axis_size("aux")
+    me = lax.axis_index("ao")
+    slots, aux_depth, _, width = blocks.shape
+    per_owner, occupied, _ = occ_coef.shape
+    flat = jnp.concatenate([pairs.reshape(-1), counts, owned_blocks])
+    used = flat.shape[0]
+    meta = jnp.broadcast_to(jnp.pad(flat, (0, -used % 128))[None], (8, used + -used % 128))
+    meta_all, occ_all = gather_small(groups, meta, occ_coef.reshape(per_owner * occupied, width))
+    meta_all = meta_all[:, 0]
+    all_pairs = meta_all[:, :2 * slots].reshape(groups, slots, 2)
+    all_counts = meta_all[:, 2 * slots]
+    all_owned = meta_all[:, 2 * slots + 1:used].reshape(-1)
+    occ_all = occ_all.reshape(groups * per_owner, occupied, width)
+
+    slot_ids = jnp.arange(slots, dtype=jnp.int32)
+    in_use = slot_ids < counts[0]
+    occ_pick = occ_all[block_place(pairs[:, 0], all_owned)]
+    half = jnp.einsum("sim,spmn->spin", occ_pick, blocks, preferred_element_type=jnp.float32)
+    half = jnp.where(in_use[:, None, None, None], half, 0.0).astype(jnp.bfloat16)
+    half = half.reshape(slots, 2, aux_depth * occupied // 2, width)
+
+    place = block_place(all_pairs[:, :, 1], all_owned)
+    live = slot_ids[None, :] < all_counts[:, None]
+    owner, local = place // per_owner, place % per_owner
+    same = (owner[:, :, None] == owner[:, None, :]) & live[:, None, :]
+    rank = jnp.sum(jnp.where(same & (slot_ids[None, None, :] < slot_ids[None, :, None]), 1, 0), axis=-1)
+    ranks = jnp.arange(CAP, dtype=jnp.int32)
+    mine = live & (owner == me)
+    positions = jnp.arange(per_owner, dtype=jnp.int32)
+    hit = live[None, None] & (place[None, None] == (
+        jnp.arange(groups, dtype=jnp.int32)[:, None] * per_owner + positions)[:, :, None, None])
+    seen = jnp.any(hit, axis=(2, 3))
+    most = jnp.max(jnp.sum(jnp.where(seen, 1, 0), axis=1))
+    my_seen = jnp.any(mine[None] & (local[None] == positions[:, None, None]), axis=(1, 2))
+    order = jnp.sum(jnp.where(my_seen[None, :] & (positions[None, :] < positions[:, None]), 1, 0), axis=1)
+    listed = my_seen[None, :] & (order[None, :] == positions[:, None])
+    pick = jnp.sum(jnp.where(listed, positions[None, :], 0), axis=1)
+    spot = jnp.sum(jnp.where(local[:, :, None] == positions, order, 0), axis=-1)
+    weights = (
+        mine[None, :, None, :]
+        & (spot[None, :, None, :] == positions[:, None, None, None])
+        & (rank[None, :, None, :] == ranks[None, None, :, None])
+    )
+    weights = jnp.sum(jnp.where(weights, 1.0, 0.0), axis=-1).reshape(-1)
+    my_owner, my_live, my_rank = (jnp.take(v, me, axis=0) for v in (owner, live, rank))
+    chosen = (
+        my_live[None, None, :]
+        & (my_owner[None, None, :] == jnp.arange(groups, dtype=jnp.int32)[:, None, None])
+        & (my_rank[None, None, :] == ranks[None, :, None])
+    )
+    idx = jnp.sum(jnp.where(chosen, slot_ids, 0), axis=-1).reshape(-1)
+    few = few_blocks(per_owner)
+    vir3 = vir_coef.reshape(per_owner, width, vir_coef.shape[1])
+    out = lax.cond(
+        most <= few,
+        functools.partial(fused, groups, nz, few, 1),
+        functools.partial(fused, groups, nz, per_owner, 2),
+        idx, weights, pick, half, vir3,
+    )
+    return out.reshape(-1, occupied, vir_coef.shape[1])
+
+
+def per_device_general(blocks, pairs, counts, owned_blocks, occ_coef, vir_coef):
     groups = lax.axis_size("ao")
     own_index = lax.axis_index("ao")
     slot_count = blocks.shape[0]
@@ -23,8 +377,7 @@
         lax.all_gather(owned_blocks, "ao", axis=0, tiled=True),
     )
     occ_all = lax.all_gather(occ_coef, "ao", axis=0, tiled=True)
-    total_blocks = all_owned.shape[0]
-    per_owner = total_blocks // groups
+    per_owner = all_owned.shape[0] // groups
     slot_ids = jnp.arange(slot_count, dtype=jnp.int32)
     in_use = slot_ids < counts[0]
     occ_pick = occ_all[block_place(pairs[:, 0], all_owned)]
@@ -50,8 +403,8 @@
         "ao",
         scatter_dimension=0,
         tiled=True,
-    ).astype(jnp.float32)
-    return result.reshape(share // occupied, occupied, vir_coef.shape[1]).astype(jnp.bfloat16)
+    )
+    return result.reshape(share // occupied, occupied, vir_coef.shape[1])
 
 
 def solution(mesh):
@@ -64,6 +417,6 @@
         P("ao", "aux"),
     )
     out_specs = P("ao", None, "aux")
-    return jax.shard_map(
-        per_device, mesh=mesh, in_specs=in_specs, out_specs=out_specs, check_vma=False
-    )
+    small = mesh.shape["ao"] == 8 and mesh.shape["aux"] == 4
+    body = per_device if small else per_device_general
+    return jax.shard_map(body, mesh=mesh, in_specs=in_specs, out_specs=out_specs, check_vma=False)

time: 291 us -> 133 us (0.46)
  waiting for transfers between devices: 210 us -> 0 us
  Pallas kernels: 0 us -> 112 us
  blocking collectives: 26.7 us -> 0 us
  matrix products: 32.1 us -> 6.31 us
  between operations: 14.5 us -> 1.42 us
  other arithmetic: 0.49 us -> 4.35 us
    all_gather x2 -> x0, waiting for transfers between devices: 135 us -> none  [the longest x1 98 us: per_device(): rows_whole = lax.all_gather(rows_local, 'aux', axis=0, tiled=True)]
    pallas_call x0 -> x2, Pallas kernels: none -> 112 us  [the longest x1 103 us: fused(): pl.pallas_call(functools.partial(main_kernel, n, nz, kept), out_shape=jax...]
    reduce_scatter x1 -> x0, waiting for transfers between devices: 75.3 us -> none  [per_device(): lax.psum_scatter(jnp.dot(rows_whole, vir_coef, preferred_element_type=jnp...]
    dot_general x2 -> x0, matrix products: 24.9 us -> none  [the longest x1 18.4 us: per_device(): jnp.dot(rows_whole, vir_coef, preferred_element_type=jnp.float32)]
    all_gather x2 -> x0, blocking collectives: 17.2 us -> none  [the longest x1 8.6 us: per_device(): occ_all = lax.all_gather(occ_coef, 'ao', axis=0, tiled=True)]
    unnamed x1 -> x0, blocking collectives: 9.49 us -> none
  transfers between devices with their start and end apart: 3 -> 0, of which waited for: 3 -> 0; matrix products, arithmetic and copies ran while one was open for 0% -> 0% of each run, Pallas kernels for 0% -> 0%
where the time goes in v1:
time: 133 us; the launch traced here: 132 us
  Pallas kernels  112 us (84%)
  local copies, waits for them, and re-layouts  7.93 us (6%)
  matrix products  6.31 us (5%)
  other arithmetic  4.35 us (3%)
  between operations  1.42 us (1%)
    pallas_call x1, Pallas kernels, fused(): pl.pallas_call(functools.partial(main_kernel, n, nz, kept), out_shape=jax...  103 us
    pallas_call x1, Pallas kernels, gather_small(): pl.pallas_call(functools.partial(small_kernel, n), out_shape=(jax.ShapeDt...  9.03 us
    dot_general x1, matrix products, per_device(): jnp.einsum('sim,spmn->spin', occ_pick, blocks, preferred_element_type=jnp...  6.31 us

profile of v1, /device:TPU:0, one launch (start us, length us, event | category | flops | bytes accessed | tf_op | source)
XLA Modules:
  0.0 132.5 jit_solution(7763353427875726120)
XLA Ops:
  0.7 0.7 slice_bitcast_fusion
  1.4 0.8 copy.90
  2.3 0.7 pad_add_fusion
  3.0 0.6 broadcast_in_dim.173.meta_ref
  3.7 9.0 %shard_map.72 = (s32[8,8,128]{2,1,0:T(8,128)}, bf16[8,80,128]{2,1,0:T(8,128)(2,1)}) custom-call(s32[8,128]{1,0:T(8,128)} %broadcast_in_dim.173.meta_ref, bf16[80,128]{1,0:T(8,128)(2,1)} %bitcast.79), custom_call_target="tpu_custom_call" | custom-call | tf_op jit(solution)/shard_map/pallas_call | solution.py:51
  12.7 0.8 slice.18
  13.5 0.2 slice_reduce_fusion
  13.8 0.2 select_reduce_fusion.14
  14.0 1.5 %gather_fusion = bf16[6,8,128]{2,1,0:T(8,128)(2,1)S(1)} fusion(bf16[80,8,128]{2,1,0:T(8,128)(2,1)} %bitcast.81, s32[1024]{0:T(1024)S(1)} %pad_clamp_fusion), kind=kCustom, calls=%fused_computation | custom fusion | bytes 24600 | tf_op jit(solution)/shard_map/gather | solution.py:321
  15.6 0.2 select_reduce_fusion.11
  16.2 0.6 reduce_max.9
  17.7 0.2 select_reduce_fusion.10
  17.9 0.2 select_reduce_fusion.12
  18.4 6.3 %fusion.6 = bf16[6,64,8,128]{3,2,1,0:T(8,128)(2,1)S(1)} fusion(bf16[6,64,128,128]{3,2,1,0:T(8,128)(2,1)} %param.10, pred[6]{0:T(512)(128)(4,1)S(1)} %iota_compare_fusion.3, bf16[6,8,128]{2,1,0:T(8,128)(2,1)S(1)} %gather_fusion), kind=kOutput, calls=%fused_computation.44 | convolution fusion | flops 101449728 | bytes 13381638 | tf_op jit(solution)/shard_map/sim,spmn->spin/dot_general | solution.py:322
  24.7 106.7 %conditional.1 = (bf16[32,8,2304]{2,1,0:T(8,128)(2,1)S(1)}) conditional(s32[]{:T(128)} %convert_element_type.9, (s32[]{:T(128)}, s32[8]{0:T(128)S(1)}, s32[8,6]{1,0:T(8,128)S(1)}, s32[6]{0:T(128)S(1)}, s32[8,1,6]{2,0,1:T(8,128)S(1)}, /*index=5*/s32[6]{0:T(128)S(1)}, s32[1,3,6]{2,1,0:T(4,128)S(1)}, s32[8,3,6]{2,0,1:T(8,128)S(1)}, ...), branch_computations={%region_8.14_spmd.clone, %region_13.19_spmd.clone} | conditional | flops 8706 | bytes 17822 | solution.py:358
  25.0 0.7 select_reduce_fusion.9.pick_ref
  25.8 0.1 and_bitcast_fusion.4
  25.9 0.1 select_reduce_fusion.7
  26.3 0.6 reshape.328.idx_ref
  26.9 0.3 select_reduce_fusion.6
  27.4 0.1 copy.89
  27.5 0.7 reshape.329.w_ref
  28.3 103.2 %branch_1_fun.2 = bf16[256,2304]{1,0:T(8,128)(2,1)S(1)} custom-call(s32[24]{0:T(128)} %reshape.328.idx_ref, f32[240]{0:T(256)} %reshape.329.w_ref, s32[10]{0:T(128)} %select_reduce_fusion.9.pick_ref, bf16[6,2,256,128]{3,2,1,0:T(8,128)(2,1)S(1)} %bitcast.65, bf16[10,128,2304]{2,1,0:T(8,128)(2,1)} %bitcast.63), custom_call_target="tpu_custom_call" | custom-call | tf_op jit(solution)/shard_map/cond/branch_1_fun/pallas_call | solution.py:269
  131.4 1.0 copy.106
  (48 shorter events, 1.9 us)
